TPU v7x, 32 devices: a whole 2x2x4 slice. The times are simulated.
32 devices in a mesh: ctx: 4 (over x, core), head: 8 (over z, y).
Axes of the slice: x: 2, y: 2, z: 4, core: 2. Of those that a mesh axis runs over, the one named last changes fastest.
Arguments:
- layer_input: bfloat16 [1024, 8192], P('ctx'), may hold values from -6 to 6
- output_grad: bfloat16 [1024, 8192], P('ctx'), may hold values from -6 to 6
- routes: int32 [1024, 8], P('ctx'), may hold values from 0 to 31, all different within a row; in each aligned block of 256 rows (0 to 255, 256 to 511, ...) at most 128 rows name the same one
- route_gates: float32 [1024, 8], P('ctx'), may hold values from 0.05 to 0.3
- query_weight: bfloat16 [40, 8192, 128], P('head', 'ctx'), may hold values from -0.0625 to 0.0625
- output_weight: bfloat16 [40, 8192, 128], P('head', 'ctx'), may hold values from -0.0625 to 0.0625
- key_values: bfloat16 [8, 1024, 128], P('head', 'ctx'), may hold values from -96 to 96
Outputs:
- input_grad: bfloat16 [1024, 8192], P('ctx', 'head')
- keyvalue_grad: float32 [8, 1024, 128], P('head', 'ctx')
Inputs may be any that keep to these rules, and one draw needn't show every extreme that they name: `routes`: each row names 8 different experts; in the 256 rows of one ctx block no expert is named more than 128 times, and some expert reaches 128.
All inputs are finite; a program needn't handle non-finite values.
Results may differ from a plain program's by a relative error of at most 0.015.
The roundings to bfloat16 on the way count: a program that leaves them out, or rounds other values in their place, can miss the bound.
Values may be sent and summed in bfloat16 or wider, within the bound.
A program may use at most 128 MiB of HBM per device.

v0:
```python
import jax
import jax.numpy as jnp
from jax import lax
from jax.sharding import PartitionSpec as P

PRECISE = lax.Precision.HIGHEST


def swapped(value, axis, bit):
    mask = 2**bit
    pairs = [(source, source ^ mask) for source in range(lax.axis_size(axis))]
    return lax.ppermute(value, axis, pairs)


def slot_table(route_rows, first_id, expert_count, slot_count):
    expert_ids = first_id + jnp.arange(expert_count, dtype=jnp.int32)
    matches = route_rows[:, :, None] == expert_ids[None, None, :]
    member = jnp.any(matches, axis=1).astype(jnp.int32)
    placed = jnp.cumsum(member, axis=0) - 1
    slot_map = (placed.T[:, None, :] == jnp.arange(slot_count, dtype=jnp.int32)[None, :, None]) & (
        member.T[:, None, :] == 1
    )
    return slot_map.astype(jnp.float32)


def expert_gate(route_rows, gate_rows, first_id, expert_count):
    expert_ids = first_id + jnp.arange(expert_count, dtype=jnp.int32)
    matches = route_rows[:, :, None] == expert_ids[None, None, :]
    return jnp.sum(
        jnp.where(matches, gate_rows[:, :, None], jnp.zeros_like(gate_rows)[:, :, None]), axis=1
    )


def attend(queries, query_place, key_rows, value_rows, key_place, head_grads):
    score_scale = queries.shape[1] ** (-0.5)
    scores = jnp.dot(queries, key_rows.T, preferred_element_type=jnp.float32) * score_scale
    scores = jnp.where(key_place[None, :] <= query_place[:, None], scores, -1e30)
    row_max = jnp.max(scores, axis=1, keepdims=True)
    raised = jnp.exp(scores - row_max)
    shares = raised / jnp.sum(raised, axis=1, keepdims=True)
    shares_low = shares.astype(jnp.bfloat16)
    outputs = jnp.dot(shares_low, value_rows, preferred_element_type=jnp.float32)
    share_grad = jnp.dot(head_grads, value_rows.T, preferred_element_type=jnp.float32)
    row_delta = jnp.sum(head_grads.astype(jnp.float32) * outputs, axis=1, keepdims=True)
    score_grad = (shares * (share_grad - row_delta) * score_scale).astype(jnp.bfloat16)
    query_grad = jnp.dot(score_grad, key_rows, preferred_element_type=jnp.float32).astype(
        jnp.bfloat16
    )
    key_grad = jnp.dot(score_grad.T, queries, preferred_element_type=jnp.float32)
    value_grad = jnp.dot(shares_low.T, head_grads, preferred_element_type=jnp.float32)
    return (query_grad, key_grad, value_grad)


def per_device(
    layer_input, output_grad, routes, route_gates, query_weight, output_weight, key_values
):
    tokens_here = layer_input.shape[0]
    per_block = query_weight.shape[0]
    expert_count = per_block - 1
    head_width = query_weight.shape[2]
    ctx_count = lax.axis_size("ctx")
    head_count = lax.axis_size("head")
    slot_count = 2 * tokens_here * routes.shape[1] // (expert_count * head_count)
    ctx_index = lax.axis_index("ctx")
    head_index = lax.axis_index("head")
    token_place = (ctx_index * tokens_here + jnp.arange(tokens_here, dtype=jnp.int32)).astype(
        jnp.float32
    )
    key_place = jnp.arange(tokens_here * ctx_count, dtype=jnp.int32).astype(jnp.float32)
    first_id = head_index * expert_count
    tables = slot_table(routes, first_id, expert_count, slot_count)
    tables_low = tables.astype(jnp.bfloat16)
    token_gates = expert_gate(routes, route_gates, first_id, expert_count)
    is_even = head_index % 2 == 0
    own_rows = key_values[0]
    partner_rows = swapped(own_rows, "head", 0)
    key_rows, value_rows = (
        lax.all_gather(jnp.where(is_even, own_rows, partner_rows), "ctx", axis=0, tiled=True),
        lax.all_gather(jnp.where(is_even, partner_rows, own_rows), "ctx", axis=0, tiled=True),
    )
    query_full, output_full = (
        lax.all_gather(query_weight, "ctx", axis=1, tiled=True),
        lax.all_gather(output_weight, "ctx", axis=1, tiled=True),
    )
    picked_input = jnp.einsum(
        "jct,td->jcd", tables_low, layer_input, preferred_element_type=jnp.float32
    ).astype(jnp.bfloat16)
    routed_query = jnp.einsum(
        "jcd,jde->jce", picked_input, query_full[:expert_count], preferred_element_type=jnp.float32
    ).astype(jnp.bfloat16)
    shared_query = jnp.dot(
        layer_input, query_full[expert_count], preferred_element_type=jnp.float32
    ).astype(jnp.bfloat16)
    slot_gate = jnp.einsum("jct,tj->jc", tables, token_gates, precision=PRECISE)
    picked_cotan = jnp.einsum(
        "jct,td->jcd", tables_low, output_grad, preferred_element_type=jnp.float32
    ).astype(jnp.bfloat16)
    routed_sum = jnp.einsum(
        "jcd,jde->jce", picked_cotan, output_full[:expert_count], preferred_element_type=jnp.float32
    )
    shared_sum = jnp.dot(output_grad, output_full[expert_count], preferred_element_type=jnp.float32)
    routed_cotan = (slot_gate[:, :, None] * routed_sum).astype(jnp.bfloat16)
    shared_cotan = shared_sum.astype(jnp.bfloat16)
    routed_place = jnp.einsum("jct,t->jc", tables, token_place, precision=PRECISE)
    queries = jnp.concatenate([routed_query.reshape(-1, head_width), shared_query], axis=0)
    query_place = jnp.concatenate([routed_place.reshape(-1), token_place], axis=0)
    head_grads = jnp.concatenate([routed_cotan.reshape(-1, head_width), shared_cotan], axis=0)
    query_grad, key_grad, value_grad = attend(
        queries, query_place, key_rows, value_rows, key_place, head_grads
    )
    routed_rows = expert_count * slot_count
    routed_qgrad = query_grad[:routed_rows].reshape(expert_count, slot_count, head_width)
    token_qgrad = jnp.einsum(
        "jct,jce->tje", tables_low, routed_qgrad, preferred_element_type=jnp.float32
    ).astype(jnp.bfloat16)
    every_qgrad = jnp.concatenate(
        [token_qgrad, query_grad[routed_rows:].reshape(tokens_here, 1, head_width)], axis=1
    )
    input_term = jnp.einsum(
        "tje,jde->td", every_qgrad, query_full, preferred_element_type=jnp.float32
    )
    input_grad = lax.psum_scatter(input_term, "head", scatter_dimension=1, tiled=True).astype(
        jnp.bfloat16
    )
    outgoing = jnp.where(is_even, value_grad, key_grad)
    incoming = swapped(outgoing.astype(jnp.bfloat16), "head", 0).astype(outgoing.dtype)
    joined_rows = jnp.where(is_even, key_grad, value_grad) + incoming
    kept_rows = lax.psum_scatter(
        joined_rows.astype(jnp.bfloat16), "ctx", scatter_dimension=0, tiled=True
    ).astype(jnp.float32)
    return (input_grad, kept_rows[None])


def solution(mesh):
    in_specs = (
        P("ctx", None),
        P("ctx", None),
        P("ctx", None),
        P("ctx", None),
        P("head", "ctx", None),
        P("head", "ctx", None),
        P("head", "ctx", None),
    )
    out_specs = (P("ctx", "head"), P("head", "ctx", None))
    return jax.shard_map(
        per_device, mesh=mesh, in_specs=in_specs, out_specs=out_specs, check_vma=False
    )
```

profile of v0, /device:TPU:13, one launch (start us, length us, event | category | flops | bytes accessed | tf_op | source)
XLA Modules:
  0.0 361.5 jit_solution(4751156317279246656)
XLA Ops:
  7.2 0.7 all-gather.5.cloned.1.call-update
  8.0 0.7 all-gather.3.cloned.1.call-update
  8.7 0.3 collective-permute-start
  9.1 1.2 reduce-window.6
  10.9 0.3 fusion.40
  11.2 0.4 fusion.38
  11.6 0.3 collective-permute-done
  11.9 7.4 %all_gather.15 = bf16[1024,128]{1,0:T(8,128)(2,1)S(1)} all-gather(bf16[256,128]{1,0:T(8,128)(2,1)S(1)} %get-tuple-element.2), channel_id=1, replica_groups=mesh['ctx'=4,'head'=8] {'ctx'}, dimensions={0}, use_global_device_ids=true | all-gather | bytes 327680 | tf_op jit(solution)/shard_map/all_gather | solution.py:79
  19.4 7.2 %all_gather.13 = bf16[1024,128]{1,0:T(8,128)(2,1)S(1)} all-gather(bf16[256,128]{1,0:T(8,128)(2,1)S(1)} %get-tuple-element.3), channel_id=1, replica_groups=mesh['ctx'=4,'head'=8] {'ctx'}, dimensions={0}, use_global_device_ids=true | all-gather | bytes 327680 | tf_op jit(solution)/shard_map/all_gather | solution.py:78
  26.6 55.7 %all-gather.5.cloned.1.call-done = bf16[5,8192,128]{2,1,0:T(8,128)(2,1)} async-done(((bf16[5,2048,128]{2,1,0:T(8,128)(2,1)}), bf16[5,8192,128]{2,1,0:T(8,128)(2,1)}) %all-gather.5.cloned.1.call-update) | async-done | bytes 10485776 | tf_op jit(solution)/shard_map/all_gather | solution.py:83
  82.3 4.1 %fusion.33 = bf16[256,128]{1,0:T(8,128)(2,1)S(1)} fusion(bf16[256,8192]{1,0:T(8,128)(2,1)} %param.8, bf16[5,8192,128]{2,1,0:T(8,128)(2,1)} %all-gather.5.cloned.1.call-done), kind=kOutput, calls=%fused_computation.28 | convolution fusion | flops 536903680 | bytes 6356992 | tf_op jit(solution)/shard_map/dot_general | solution.py:101
  86.6 9.6 %fusion.22 = bf16[4,128,128]{2,1,0:T(8,128)(2,1)S(1)} fusion(bf16[5,8192,128]{2,1,0:T(8,128)(2,1)} %all-gather.5.cloned.1.call-done, bf16[256,8192]{1,0:T(8,128)(2,1)} %param.8, s32[4,256]{1,0:T(4,128)S(1)} %bitcast.78, pred[4,256]{1,0:T(4,128)(4,1)S(1)} %broadcast_compare_fusion, f32[4,128]{1,0:T(4,128)S(1)} %bitcast.84), kind=kOutput, calls=%fused_computation.25 | convolution fusion | flops 3226075136 | bytes 12721152 | tf_op jit(solution)/shard_map/jcd,jde->jce/dot_general | solution.py:98
  96.3 58.2 %all-gather.3.cloned.1.call-done = bf16[5,8192,128]{2,1,0:T(8,128)(2,1)} async-done(((bf16[5,2048,128]{2,1,0:T(8,128)(2,1)}), bf16[5,8192,128]{2,1,0:T(8,128)(2,1)}) %all-gather.3.cloned.1.call-update) | async-done | bytes 10485776 | tf_op jit(solution)/shard_map/all_gather | solution.py:82
  154.5 4.1 %fusion.32 = bf16[256,128]{1,0:T(8,128)(2,1)S(1)} fusion(bf16[256,8192]{1,0:T(8,128)(2,1)} %param.7, bf16[5,8192,128]{2,1,0:T(8,128)(2,1)} %all-gather.3.cloned.1.call-done), kind=kOutput, calls=%fused_computation.27 | convolution fusion | flops 536903680 | bytes 6356992 | tf_op jit(solution)/shard_map/dot_general | solution.py:91
  158.6 9.4 %fusion.27 = bf16[4,128,128]{2,1,0:T(8,128)(2,1)S(1)} fusion(bf16[5,8192,128]{2,1,0:T(8,128)(2,1)} %all-gather.3.cloned.1.call-done, bf16[256,8192]{1,0:T(8,128)(2,1)} %param.7, s32[4,256]{1,0:T(4,128)S(1)} %bitcast.79, pred[4,256]{1,0:T(4,128)(4,1)S(1)} %broadcast_compare_fusion), kind=kOutput, calls=%fused_computation.26 | convolution fusion | flops 3226009600 | bytes 12719104 | tf_op jit(solution)/shard_map/jcd,jde->jce/dot_general | solution.py:88
  168.0 0.7 fusion.14
  168.7 0.9 fusion.7
  169.6 0.8 fusion.6
  170.5 0.7 fusion.21
  171.1 0.8 multiply_convert_fusion
  172.0 0.6 convolution_convert_fusion.3
  172.5 0.6 fusion.59
  173.2 0.6 select_convert_fusion
  173.8 0.3 collective-permute-start.1
  174.1 0.3 fusion.15
  174.4 7.0 %collective-permute-done.1 = bf16[1024,128]{1,0:T(8,128)(2,1)S(1)} collective-permute-done((bf16[1024,128]{1,0:T(8,128)(2,1)S(1)}, bf16[1024,128]{1,0:T(8,128)(2,1)S(1)}, u32[]{:S(2)}, u32[]{:S(2)}) %collective-permute-start.1) | collective-permute-done | bytes 262176 | tf_op jit(solution)/shard_map/ppermute | solution.py:12
  181.5 0.8 add_convert_fusion
  182.3 12.7 %convolution_bitcast_fusion = f32[256,8192]{1,0:T(8,128)} fusion(bf16[5,8192,128]{2,1,0:T(8,128)(2,1)} %all-gather.3.cloned.1.call-done, bf16[256,1,128]{2,0,1:T(8,128)(2,1)S(1)} %slice_bitcast_fusion.8, bf16[256,4,128]{2,0,1:T(8,128)(2,1)S(1)} %fusion.15), kind=kOutput, calls=%fused_computation.2 | convolution fusion | flops 2684518400 | bytes 19202048 | tf_op jit(solution)/shard_map/tje,jde->td/dot_general | solution.py:119
  195.1 7.6 %reduce-scatter.5.cloned.1.call-done = bf16[256,128]{1,0:T(8,128)(2,1)} async-done(((bf16[1024,128]{1,0:T(8,128)(2,1)}), bf16[256,128]{1,0:T(8,128)(2,1)}) %reduce-scatter.5.cloned.1.call-update) | async-done | bytes 65552 | tf_op jit(solution)/shard_map/reduce_scatter | solution.py:128
  202.7 1.5 bitcast_convert_fusion
  204.2 148.7 %reduce-scatter.3.cloned.1.call-done = f32[256,1024]{1,0:T(8,128)} async-done(((f32[256,8192]{1,0:T(8,128)}), f32[256,1024]{1,0:T(8,128)}) %reduce-scatter.3.cloned.1.call-update) | async-done | bytes 1048592 | tf_op jit(solution)/shard_map/reduce_scatter | solution.py:122
  352.9 2.1 convert_element_type.91
  (33 shorter events, 1.1 us)
Async XLA Ops:
  7.2 1.6 copy-start
  7.2 1.9 copy-start.1
  7.2 3.6 copy-start.2
  7.2 75.1 %all-gather.5.cloned.1.call-start = ((), (), s32[]{:S(2)}) async-start(), calls=%async_computation.3 | async-start | bytes 13107200 | tf_op jit(solution)/shard_map/all_gather | solution.py:83
  7.9 146.5 %all-gather.3.cloned.1.call-start = ((), (), s32[]{:S(2)}) async-start(), calls=%async_computation.2 | async-start | bytes 13107200 | tf_op jit(solution)/shard_map/all_gather | solution.py:82
  8.7 194.0 %reduce-scatter.5.cloned.1.call-start = ((), (), s32[]{:S(2)}) async-start(), calls=%async_computation.5 | async-start | bytes 327680 | tf_op jit(solution)/shard_map/reduce_scatter | solution.py:128
  8.7 3.2 collective-permute-start
  173.8 7.7 %collective-permute-start.1 = (bf16[1024,128]{1,0:T(8,128)(2,1)S(1)}, bf16[1024,128]{1,0:T(8,128)(2,1)S(1)}, u32[]{:S(2)}, u32[]{:S(2)}) collective-permute-start(bf16[1024,128]{1,0:T(8,128)(2,1)S(1)} %get-tuple-element.6), channel_id=1, source_target_pairs={{0,1},{1,0},{2,3},{3,2},{4,5},{5,4},{6,7},{7,6},{8,9},{9,8},{10,11... | collective-permute-start | bytes 786440 | tf_op jit(solution)/shard_map/ppermute | solution.py:12
  182.3 170.6 %reduce-scatter.3.cloned.1.call-start = ((), (), s32[]{:S(2)}) async-start(), calls=%async_computation.4 | async-start | bytes 9437184 | tf_op jit(solution)/shard_map/reduce_scatter | solution.py:122
Sparse Core Ops, SparseCore 0:
  9.6 72.7 all-gather.4
  83.9 70.5 all-gather.2
  182.4 20.2 reduce-scatter.4
  206.2 146.6 reduce-scatter.2
where the time goes:
time: 365 us; the launch traced here: 361 us
  waiting for transfers between devices  279 us (76%)
  matrix products  44.9 us (12%)
  blocking collectives  14.7 us (4%)
  between operations  13.9 us (4%)
  other arithmetic  7.71 us (2%)
    reduce_scatter x1, waiting for transfers between devices, per_device(): lax.psum_scatter(input_term, 'head', scatter_dimension=1, tiled=True)  149 us
    all_gather x1, waiting for transfers between devices, per_device(): lax.all_gather(query_weight, 'ctx', axis=1, tiled=True)  58.2 us
    all_gather x1, waiting for transfers between devices, per_device(): lax.all_gather(output_weight, 'ctx', axis=1, tiled=True)  55.7 us
    dot_general x1, matrix products, per_device(): jnp.einsum('tje,jde->td', every_qgrad, query_full, preferred_element_type...  12.7 us
    dot_general x1, matrix products, per_device(): jnp.einsum('jcd,jde->jce', picked_cotan, output_full[:expert_count], pref...  9.59 us
    dot_general x1, matrix products, per_device(): jnp.einsum('jcd,jde->jce', picked_input, query_full[:expert_count], prefe...  9.42 us
    reduce_scatter x1, waiting for transfers between devices, per_device(): lax.psum_scatter(joined_rows.astype(jnp.bfloat16), 'ctx', scatter_dimensi...  7.64 us
    all_gather x1, blocking collectives, per_device(): lax.all_gather(jnp.where(is_even, partner_rows, own_rows), 'ctx', axis=0,...  7.44 us
  transfers between devices with their start and end apart: 6, of which 6 were waited for; matrix products, arithmetic and copies ran while one was open for 9% of the time, Pallas kernels for 0%

commit v1 on v0

--- a/solution.py
+++ b/solution.py
@@ -1,15 +1,234 @@
+import functools
+
 import jax
 import jax.numpy as jnp
 from jax import lax
+from jax.experimental import pallas as pl
+from jax.experimental.pallas import tpu as pltpu
 from jax.sharding import PartitionSpec as P
 
 PRECISE = lax.Precision.HIGHEST
 
 
-def swapped(value, axis, bit):
-    mask = 2**bit
-    pairs = [(source, source ^ mask) for source in range(lax.axis_size(axis))]
-    return lax.ppermute(value, axis, pairs)
+MESH = pl.DeviceIdType.MESH
+ANY = pl.BlockSpec(memory_space=pl.ANY)
+
+
+def partner(step, flip):
+    ctx, ctx_count = lax.axis_index("ctx"), lax.axis_size("ctx")
+    head = lax.axis_index("head")
+    other = head + flip * (1 - 2 * (head % 2))
+    return lax.rem(ctx + step, ctx_count), other
+
+
+def paired_steps(ctx_count):
+    return [(step, flip) for step in range(ctx_count) for flip in range(2) if step or flip]
+
+
+def remote(source, target, send, recv, ctx, head):
+    return pltpu.make_async_remote_copy(
+        src_ref=source,
+        dst_ref=target,
+        send_sem=send,
+        recv_sem=recv,
+        device_id=(ctx, head),
+        device_id_type=MESH,
+    )
+
+
+def greet(places):
+    barrier = pltpu.get_barrier_semaphore()
+    for place in places:
+        pl.semaphore_signal(barrier, inc=1, device_id=place, device_id_type=MESH)
+    pl.semaphore_wait(barrier, len(places))
+
+
+def gather_kernel(
+    pieces,
+    query_ref,
+    output_ref,
+    pair_ref,
+    query_out,
+    output_out,
+    pair_out,
+    stage,
+    load_sem,
+    store_sem,
+    side_send,
+    side_recv,
+    far_send,
+    far_recv,
+    hand_send,
+    hand_recv,
+    pair_send,
+    pair_recv,
+    pair_store,
+):
+    ctx_count = lax.axis_size("ctx")
+    ctx, head = lax.axis_index("ctx"), lax.axis_index("head")
+    chips = ctx_count // 2
+    core = ctx % 2
+    chip = ctx // 2
+    sibling = ctx + 1 - 2 * core
+    heads, depth, _ = query_ref.shape
+    span = heads // pieces
+    tokens = pair_ref.shape[1]
+    sources, targets = (query_ref, output_ref), (query_out, output_out)
+    chunks = [(which, piece) for which in range(2) for piece in range(pieces)]
+
+    def staged(which, piece):
+        return stage.at[which, pl.ds(piece * span, span)]
+
+    def placed(which, piece, owner):
+        return targets[which].at[
+            pl.ds(piece * span, span), pl.ds(pl.multiple_of(owner * depth, depth), depth)
+        ]
+
+    loads = []
+    for k, (which, piece) in enumerate(chunks):
+        load = pltpu.make_async_copy(
+            sources[which].at[pl.ds(piece * span, span)], staged(which, piece), load_sem.at[k]
+        )
+        load.start()
+        loads.append(load)
+    steps = paired_steps(ctx_count)
+    greet([partner(step, flip) for step, flip in steps])
+
+    far, ends = {}, []
+    for k, (which, piece) in enumerate(chunks):
+        loads[k].wait()
+        for hop in range(1, chips):
+            copy = remote(
+                staged(which, piece),
+                placed(which, piece, ctx),
+                far_send.at[k, hop - 1],
+                far_recv.at[k, hop - 1],
+                lax.rem(chip + hop, chips) * 2 + core,
+                head,
+            )
+            copy.start()
+            far[k, hop] = copy
+        side = remote(
+            staged(which, piece),
+            placed(which, piece, ctx),
+            side_send.at[k],
+            side_recv.at[k],
+            sibling,
+            head,
+        )
+        side.start()
+        store = pltpu.make_async_copy(
+            staged(which, piece), placed(which, piece, ctx), store_sem.at[k]
+        )
+        store.start()
+        ends += [side, store]
+
+    mine = pair_out.at[head % 2, pl.ds(pl.multiple_of(ctx * tokens, tokens), tokens)]
+    for n, (step, flip) in enumerate(steps):
+        copy = remote(
+            pair_ref.at[0], mine, pair_send.at[n], pair_recv.at[n], *partner(step, flip)
+        )
+        copy.start()
+        ends.append(copy)
+    store = pltpu.make_async_copy(pair_ref.at[0], mine, pair_store)
+    store.start()
+    ends.append(store)
+
+    for k, (which, piece) in enumerate(chunks):
+        for hop in range(1, chips):
+            far[k, hop].wait_recv()
+            owner = lax.rem(chip - hop + chips, chips) * 2 + core
+            block = placed(which, piece, owner)
+            hand = remote(
+                block, block, hand_send.at[k, hop - 1], hand_recv.at[k, hop - 1], sibling, head
+            )
+            hand.start()
+            ends.append(hand)
+    for copy in far.values():
+        copy.wait_send()
+    for copy in ends:
+        copy.wait()
+
+
+def gather_all(query_weight, output_weight, key_values):
+    heads, depth, width = query_weight.shape
+    ctx_count = lax.axis_size("ctx")
+    chips = ctx_count // 2
+    pieces = heads if chips <= 2 else 1
+    full = jax.ShapeDtypeStruct((heads, depth * ctx_count, width), query_weight.dtype)
+    pair = jax.ShapeDtypeStruct((2, key_values.shape[1] * ctx_count, width), key_values.dtype)
+    count, hops, others = 2 * pieces, max(chips - 1, 1), 2 * ctx_count - 1
+    dma = pltpu.SemaphoreType.DMA
+    return pl.pallas_call(
+        functools.partial(gather_kernel, pieces),
+        out_shape=(full, full, pair),
+        in_specs=[ANY, ANY, pl.BlockSpec(memory_space=pltpu.VMEM)],
+        out_specs=(ANY, ANY, ANY),
+        scratch_shapes=[pltpu.VMEM((2, heads, depth, width), query_weight.dtype)]
+        + [dma((count,))] * 4
+        + [dma((count, hops))] * 4
+        + [dma((others,))] * 2
+        + [dma],
+        compiler_params=pltpu.CompilerParams(collective_id=0, has_side_effects=True),
+    )(query_weight, output_weight, key_values)
+
+
+def exchange_kernel(
+    term_ref, grads_ref, term_out, grads_out, term_send, term_recv, grads_send, grads_recv
+):
+    ctx_count, head_count = lax.axis_size("ctx"), lax.axis_size("head")
+    ctx, head = lax.axis_index("ctx"), lax.axis_index("head")
+    columns = term_ref.shape[1] // head_count
+    steps = paired_steps(ctx_count)
+    others = [lax.rem(head + step, head_count) for step in range(1, head_count)]
+    greet([(ctx, other) for other in others] + [partner(step, flip) for step, flip in steps])
+    copies = []
+    for n, other in enumerate(others):
+        copies.append(
+            remote(
+                term_ref.at[:, pl.ds(pl.multiple_of(other * columns, columns), columns)],
+                term_out.at[n],
+                term_send.at[n],
+                term_recv.at[n],
+                ctx,
+                other,
+            )
+        )
+        copies[-1].start()
+    for n, (step, flip) in enumerate(steps):
+        to_ctx, to_head = partner(step, flip)
+        copies.append(
+            remote(
+                grads_ref.at[to_head % 2, to_ctx],
+                grads_out.at[n],
+                grads_send.at[n],
+                grads_recv.at[n],
+                to_ctx,
+                to_head,
+            )
+        )
+        copies[-1].start()
+    for copy in copies:
+        copy.wait()
+
+
+def exchange(term, grads):
+    ctx_count, head_count = lax.axis_size("ctx"), lax.axis_size("head")
+    others = 2 * ctx_count - 1
+    dma = pltpu.SemaphoreType.DMA
+    return pl.pallas_call(
+        exchange_kernel,
+        out_shape=(
+            jax.ShapeDtypeStruct(
+                (head_count - 1, term.shape[0], term.shape[1] // head_count), term.dtype
+            ),
+            jax.ShapeDtypeStruct((others,) + grads.shape[2:], grads.dtype),
+        ),
+        in_specs=[ANY, ANY],
+        out_specs=(ANY, ANY),
+        scratch_shapes=[dma((head_count - 1,))] * 2 + [dma((others,))] * 2,
+        compiler_params=pltpu.CompilerParams(collective_id=1, has_side_effects=True),
+    )(term, grads)
 
 
 def slot_table(route_rows, first_id, expert_count, slot_count):
@@ -71,17 +290,8 @@
     tables = slot_table(routes, first_id, expert_count, slot_count)
     tables_low = tables.astype(jnp.bfloat16)
     token_gates = expert_gate(routes, route_gates, first_id, expert_count)
-    is_even = head_index % 2 == 0
-    own_rows = key_values[0]
-    partner_rows = swapped(own_rows, "head", 0)
-    key_rows, value_rows = (
-        lax.all_gather(jnp.where(is_even, own_rows, partner_rows), "ctx", axis=0, tiled=True),
-        lax.all_gather(jnp.where(is_even, partner_rows, own_rows), "ctx", axis=0, tiled=True),
-    )
-    query_full, output_full = (
-        lax.all_gather(query_weight, "ctx", axis=1, tiled=True),
-        lax.all_gather(output_weight, "ctx", axis=1, tiled=True),
-    )
+    query_full, output_full, pair_full = gather_all(query_weight, output_weight, key_values)
+    key_rows, value_rows = pair_full[0], pair_full[1]
     picked_input = jnp.einsum(
         "jct,td->jcd", tables_low, layer_input, preferred_element_type=jnp.float32
     ).astype(jnp.bfloat16)
@@ -119,15 +329,17 @@
     input_term = jnp.einsum(
         "tje,jde->td", every_qgrad, query_full, preferred_element_type=jnp.float32
     )
-    input_grad = lax.psum_scatter(input_term, "head", scatter_dimension=1, tiled=True).astype(
-        jnp.bfloat16
-    )
-    outgoing = jnp.where(is_even, value_grad, key_grad)
-    incoming = swapped(outgoing.astype(jnp.bfloat16), "head", 0).astype(outgoing.dtype)
-    joined_rows = jnp.where(is_even, key_grad, value_grad) + incoming
-    kept_rows = lax.psum_scatter(
-        joined_rows.astype(jnp.bfloat16), "ctx", scatter_dimension=0, tiled=True
-    ).astype(jnp.float32)
+    term = input_term.astype(jnp.bfloat16)
+    grads = jnp.stack([key_grad, value_grad]).astype(jnp.bfloat16)
+    grads = grads.reshape(2, ctx_count, tokens_here, head_width)
+    term_got, grads_got = exchange(term, grads)
+    columns = term.shape[1] // head_count
+    own_term = lax.dynamic_slice_in_dim(term, head_index * columns, columns, 1)
+    input_grad = (
+        own_term.astype(jnp.float32) + jnp.sum(term_got.astype(jnp.float32), axis=0)
+    ).astype(jnp.bfloat16)
+    own_grads = grads[head_index % 2, ctx_index].astype(jnp.float32)
+    kept_rows = own_grads + jnp.sum(grads_got.astype(jnp.float32), axis=0)
     return (input_grad, kept_rows[None])
 
 

time: 365 us -> 278 us (0.76)
  waiting for transfers between devices: 279 us -> 0 us
  Pallas kernels: 0 us -> 221 us
  blocking collectives: 14.7 us -> 0 us
  between operations: 13.9 us -> 0.85 us
    pallas_call x0 -> x2, Pallas kernels: none -> 221 us  [the longest x1 124 us: gather_all(): pl.pallas_call(functools.partial(gather_kernel, pieces), out_shape=(full,...]
    reduce_scatter x2 -> x0, waiting for transfers between devices: 156 us -> none  [the longest x1 149 us: per_device(): lax.psum_scatter(input_term, 'head', scatter_dimension=1, tiled=True)]
    all_gather x2 -> x0, waiting for transfers between devices: 114 us -> none  [the longest x1 58.2 us: per_device(): lax.all_gather(query_weight, 'ctx', axis=1, tiled=True)]
    all_gather x2 -> x0, blocking collectives: 14.7 us -> none  [the longest x1 7.44 us: per_device(): lax.all_gather(jnp.where(is_even, partner_rows, own_rows), 'ctx', axis=0,...]
    ppermute x2 -> x0, waiting for transfers between devices: 7.33 us -> none  [swapped(): return lax.ppermute(value, axis, pairs)]
  transfers between devices with their start and end apart: 6 -> 0, of which waited for: 6 -> 0; matrix products, arithmetic and copies ran while one was open for 9% -> 0% of each run, Pallas kernels for 0% -> 0%
where the time goes in v1:
time: 278 us
  Pallas kernels  221 us (79%)
  matrix products  44.5 us (16%)
  other arithmetic  11.3 us (4%)
    pallas_call x1, Pallas kernels, gather_all(): pl.pallas_call(functools.partial(gather_kernel, pieces), out_shape=(full,...  124 us
    pallas_call x1, Pallas kernels, exchange(): pl.pallas_call(exchange_kernel, out_shape=(jax.ShapeDtypeStruct((head_cou...  97.1 us
    dot_general x1, matrix products, per_device(): jnp.einsum('tje,jde->td', every_qgrad, query_full, preferred_element_type...  12.1 us
    dot_general x1, matrix products, per_device(): jnp.einsum('jcd,jde->jce', picked_input, query_full[:expert_count], prefe...  9.46 us
    dot_general x1, matrix products, per_device(): jnp.einsum('jcd,jde->jce', picked_cotan, output_full[:expert_count], pref...  9.25 us

profile of v1, /device:TPU:13, one launch (start us, length us, event | category | flops | bytes accessed | tf_op | source)
XLA Modules:
  0.0 278.0 jit_solution(1890147164257900096)
XLA Ops:
  0.7 0.8 compare_reduce_fusion
  1.5 1.2 reduce-window.6
  2.7 0.8 fusion.83
  3.5 0.1 slice.40
  3.6 0.1 copy.15
  3.8 0.1 copy.16
  3.9 0.1 add_bitcast_fusion
  3.9 0.4 fusion.52
  4.3 0.4 fusion.54
  4.7 123.7 %shard_map.86 = (bf16[5,8192,128]{2,1,0:T(8,128)(2,1)}, bf16[5,8192,128]{2,1,0:T(8,128)(2,1)}, bf16[2,1024,128]{2,1,0:T(8,128)(2,1)}) custom-call(bf16[5,2048,128]{2,1,0:T(8,128)(2,1)} %query_ref.1, bf16[5,2048,128]{2,1,0:T(8,128)(2,1)} %output_ref.1, bf16[1,256,128]{2,1,0:T(8,128)(2,1)} %pair_ref.1), custom_call_target="tpu_custom_call" | custom-call | tf_op jit(solution)/shard_map/pallas_call | solution.py:162
  128.4 4.4 %fusion.43 = bf16[256,128]{0,1:T(8,128)(2,1)S(1)} fusion(bf16[256,8192]{1,0:T(8,128)(2,1)} %param.8, bf16[5,8192,128]{2,1,0:T(8,128)(2,1)} %get-tuple-element.9), kind=kOutput, calls=%fused_computation.35 | convolution fusion | flops 536903680 | bytes 6356992 | tf_op jit(solution)/shard_map/dot_general | solution.py:311
  132.8 9.2 %fusion.27 = bf16[4,128,128]{2,1,0:T(8,128)(2,1)S(1)} fusion(bf16[5,8192,128]{2,1,0:T(8,128)(2,1)} %get-tuple-element.9, bf16[256,8192]{1,0:T(8,128)(2,1)} %param.8, s32[4,256]{1,0:T(4,128)S(1)} %bitcast.98, pred[4,256]{1,0:T(4,128)(4,1)S(1)} %broadcast_compare_fusion, f32[4,128]{1,0:T(4,128)S(1)} %bitcast.106), kind=kOutput, calls=%fused_computation.31 | convolution fusion | flops 3226075136 | bytes 12721152 | tf_op jit(solution)/shard_map/jcd,jde->jce/dot_general | solution.py:308
  142.0 0.1 copy.18
  142.1 4.4 %fusion.46 = bf16[256,128]{0,1:T(8,128)(2,1)S(1)} fusion(bf16[256,8192]{1,0:T(8,128)(2,1)} %param.7, bf16[5,8192,128]{2,1,0:T(8,128)(2,1)} %get-tuple-element.7), kind=kOutput, calls=%fused_computation.36 | convolution fusion | flops 536903680 | bytes 6356992 | tf_op jit(solution)/shard_map/dot_general | solution.py:301
  146.5 0.1 copy.17
  146.6 9.5 %fusion.32 = bf16[4,128,128]{2,1,0:T(8,128)(2,1)S(1)} fusion(bf16[5,8192,128]{2,1,0:T(8,128)(2,1)} %get-tuple-element.7, bf16[256,8192]{1,0:T(8,128)(2,1)} %param.7, s32[4,256]{1,0:T(4,128)S(1)} %bitcast.99, pred[4,256]{1,0:T(4,128)(4,1)S(1)} %broadcast_compare_fusion), kind=kOutput, calls=%fused_computation.32 | convolution fusion | flops 3226009600 | bytes 12719104 | tf_op jit(solution)/shard_map/jcd,jde->jce/dot_general | solution.py:298
  156.1 0.7 fusion.19
  156.8 0.9 fusion.8
  157.8 0.8 fusion.7
  158.6 0.7 fusion.26
  159.3 0.6 convolution_convert_fusion.2
  159.9 0.8 multiply_convert_fusion
  160.7 0.6 convolution_convert_fusion.5
  161.3 0.6 convolution_convert_fusion.3
  162.0 0.3 fusion.20
  162.3 12.1 %fusion.term_ref = bf16[256,8192]{1,0:T(8,128)(2,1)} fusion(bf16[5,8192,128]{2,1,0:T(8,128)(2,1)} %get-tuple-element.7, bf16[256,1,128]{2,0,1:T(8,128)(2,1)S(1)} %slice_bitcast_fusion, bf16[256,4,128]{2,0,1:T(8,128)(2,1)S(1)} %fusion.20), kind=kOutput, calls=%fused_computation.3 | convolution fusion | flops 2686615552 | bytes 15007744 | tf_op jit(solution)/shard_map/tje,jde->td/dot_general | solution.py:329
  174.4 0.8 pad_maximum_fusion.grads_ref
  175.2 97.1 %shard_map.87 = (bf16[7,256,1024]{2,1,0:T(8,128)(2,1)}, bf16[7,256,128]{2,1,0:T(8,128)(2,1)}) custom-call(bf16[256,8192]{1,0:T(8,128)(2,1)} %fusion.term_ref, bf16[2,4,256,128]{3,2,1,0:T(8,128)(2,1)} %pad_maximum_fusion.grads_ref), custom_call_target="tpu_custom_call" | custom-call | tf_op jit(solution)/shard_map/pallas_call | solution.py:219
  272.3 2.9 %convert_reduce_fusion = f32[256,1024]{1,0:T(8,128)S(1)} fusion(bf16[7,256,1024]{2,1,0:T(8,128)(2,1)} %get-tuple-element.10), kind=kLoop, calls=%fused_computation.8 | loop fusion | flops 3407872 | bytes 4718592 | tf_op jit(solution)/shard_map/reduce_sum | solution.py:339
  275.3 2.0 add_convert_fusion
  277.3 0.1 convert_reduce_fusion.1
  277.3 0.7 convert_add_fusion
  (16 shorter events, 0.1 us)
Async XLA Ops:
  146.6 9.5 %copy-start = (bf16[2,1024,128]{2,1,0:T(8,128)(2,1)S(1)}, bf16[2,1024,128]{2,1,0:T(8,128)(2,1)}, u32[]{:S(2)}) copy-start(bf16[2,1024,128]{2,1,0:T(8,128)(2,1)} %get-tuple-element.8) | copy-start | bytes 1572868
  272.3 4.9 %copy-start.1 = (bf16[7,256,128]{2,1,0:T(8,128)(2,1)S(1)}, bf16[7,256,128]{2,1,0:T(8,128)(2,1)}, u32[]{:S(2)}) copy-start(bf16[7,256,128]{2,1,0:T(8,128)(2,1)} %get-tuple-element.11) | copy-start | bytes 1376260

commit v2 on v1

--- a/solution.py
+++ b/solution.py
@@ -174,7 +174,7 @@
 
 
 def exchange_kernel(
-    term_ref, grads_ref, term_out, grads_out, term_send, term_recv, grads_send, grads_recv
+    term_ref, grads_ref, term_out, grads_out, relay_out, term_send, term_recv, grads_send, grads_recv
 ):
     ctx_count, head_count = lax.axis_size("ctx"), lax.axis_size("head")
     ctx, head = lax.axis_index("ctx"), lax.axis_index("head")
@@ -183,7 +183,16 @@
     others = [lax.rem(head + step, head_count) for step in range(1, head_count)]
     greet([(ctx, other) for other in others] + [partner(step, flip) for step, flip in steps])
     copies = []
+    half, last = head_count // 2, head_count - 1
+    relay = lax.rem(head + head_count - half // 2, head_count)
+    opposite = pl.ds(pl.multiple_of(others[half - 1] * columns, columns), columns)
+    first = remote(
+        term_ref.at[:, opposite], relay_out, term_send.at[last], term_recv.at[last], ctx, relay
+    )
+    first.start()
     for n, other in enumerate(others):
+        if n == half - 1:
+            continue
         copies.append(
             remote(
                 term_ref.at[:, pl.ds(pl.multiple_of(other * columns, columns), columns)],
@@ -208,6 +217,18 @@
             )
         )
         copies[-1].start()
+    first.wait_recv()
+    second = remote(
+        relay_out,
+        term_out.at[half - 1],
+        term_send.at[half - 1],
+        term_recv.at[half - 1],
+        ctx,
+        relay,
+    )
+    second.start()
+    first.wait_send()
+    copies.append(second)
     for copy in copies:
         copy.wait()
 
@@ -223,10 +244,11 @@
                 (head_count - 1, term.shape[0], term.shape[1] // head_count), term.dtype
             ),
             jax.ShapeDtypeStruct((others,) + grads.shape[2:], grads.dtype),
+            jax.ShapeDtypeStruct((term.shape[0], term.shape[1] // head_count), term.dtype),
         ),
         in_specs=[ANY, ANY],
-        out_specs=(ANY, ANY),
-        scratch_shapes=[dma((head_count - 1,))] * 2 + [dma((others,))] * 2,
+        out_specs=(ANY, ANY, ANY),
+        scratch_shapes=[dma((head_count,))] * 2 + [dma((others,))] * 2,
         compiler_params=pltpu.CompilerParams(collective_id=1, has_side_effects=True),
     )(term, grads)
 
@@ -332,7 +354,7 @@
     term = input_term.astype(jnp.bfloat16)
     grads = jnp.stack([key_grad, value_grad]).astype(jnp.bfloat16)
     grads = grads.reshape(2, ctx_count, tokens_here, head_width)
-    term_got, grads_got = exchange(term, grads)
+    term_got, grads_got, _ = exchange(term, grads)
     columns = term.shape[1] // head_count
     own_term = lax.dynamic_slice_in_dim(term, head_index * columns, columns, 1)
     input_grad = (

time: 278 us -> 276 us (level)
  Pallas kernels: 221 us -> 218 us
    pallas_call x1, Pallas kernels: 97.1 us -> 94.3 us  [exchange(): pl.pallas_call(exchange_kernel, out_shape=(jax.ShapeDtypeStruct((head_cou...]
where the time goes in v2:
time: 276 us; the launch traced here: 275 us
  Pallas kernels  218 us (79%)
  matrix products  44.5 us (16%)
  other arithmetic  11.3 us (4%)
    pallas_call x1, Pallas kernels, gather_all(): pl.pallas_call(functools.partial(gather_kernel, pieces), out_shape=(full,...  124 us
    pallas_call x1, Pallas kernels, exchange(): pl.pallas_call(exchange_kernel, out_shape=(jax.ShapeDtypeStruct((head_cou...  94.3 us
    dot_general x1, matrix products, per_device(): jnp.einsum('tje,jde->td', every_qgrad, query_full, preferred_element_type...  12.1 us
    dot_general x1, matrix products, per_device(): jnp.einsum('jcd,jde->jce', picked_input, query_full[:expert_count], prefe...  9.46 us
    dot_general x1, matrix products, per_device(): jnp.einsum('jcd,jde->jce', picked_cotan, output_full[:expert_count], pref...  9.25 us

profile of v2, /device:TPU:13, one launch (start us, length us, event | category | flops | bytes accessed | tf_op | source)
XLA Modules:
  0.0 275.2 jit_solution(11670285998481257003)
XLA Ops:
  0.7 0.8 compare_reduce_fusion
  1.5 1.2 reduce-window.6
  2.7 0.8 fusion.83
  3.5 0.1 slice.40
  3.6 0.1 copy.15
  3.8 0.1 copy.16
  3.9 0.1 add_bitcast_fusion
  3.9 0.4 fusion.52
  4.3 0.4 fusion.54
  4.7 123.7 %shard_map.86 = (bf16[5,8192,128]{2,1,0:T(8,128)(2,1)}, bf16[5,8192,128]{2,1,0:T(8,128)(2,1)}, bf16[2,1024,128]{2,1,0:T(8,128)(2,1)}) custom-call(bf16[5,2048,128]{2,1,0:T(8,128)(2,1)} %query_ref.1, bf16[5,2048,128]{2,1,0:T(8,128)(2,1)} %output_ref.1, bf16[1,256,128]{2,1,0:T(8,128)(2,1)} %pair_ref.1), custom_call_target="tpu_custom_call" | custom-call | tf_op jit(solution)/shard_map/pallas_call | solution.py:162
  128.4 4.4 %fusion.43 = bf16[256,128]{0,1:T(8,128)(2,1)S(1)} fusion(bf16[256,8192]{1,0:T(8,128)(2,1)} %param.8, bf16[5,8192,128]{2,1,0:T(8,128)(2,1)} %get-tuple-element.9), kind=kOutput, calls=%fused_computation.35 | convolution fusion | flops 536903680 | bytes 6356992 | tf_op jit(solution)/shard_map/dot_general | solution.py:333
  132.8 9.2 %fusion.27 = bf16[4,128,128]{2,1,0:T(8,128)(2,1)S(1)} fusion(bf16[5,8192,128]{2,1,0:T(8,128)(2,1)} %get-tuple-element.9, bf16[256,8192]{1,0:T(8,128)(2,1)} %param.8, s32[4,256]{1,0:T(4,128)S(1)} %bitcast.98, pred[4,256]{1,0:T(4,128)(4,1)S(1)} %broadcast_compare_fusion, f32[4,128]{1,0:T(4,128)S(1)} %bitcast.106), kind=kOutput, calls=%fused_computation.31 | convolution fusion | flops 3226075136 | bytes 12721152 | tf_op jit(solution)/shard_map/jcd,jde->jce/dot_general | solution.py:330
  142.0 0.1 copy.18
  142.1 4.4 %fusion.46 = bf16[256,128]{0,1:T(8,128)(2,1)S(1)} fusion(bf16[256,8192]{1,0:T(8,128)(2,1)} %param.7, bf16[5,8192,128]{2,1,0:T(8,128)(2,1)} %get-tuple-element.7), kind=kOutput, calls=%fused_computation.36 | convolution fusion | flops 536903680 | bytes 6356992 | tf_op jit(solution)/shard_map/dot_general | solution.py:323
  146.5 0.1 copy.17
  146.6 9.5 %fusion.32 = bf16[4,128,128]{2,1,0:T(8,128)(2,1)S(1)} fusion(bf16[5,8192,128]{2,1,0:T(8,128)(2,1)} %get-tuple-element.7, bf16[256,8192]{1,0:T(8,128)(2,1)} %param.7, s32[4,256]{1,0:T(4,128)S(1)} %bitcast.99, pred[4,256]{1,0:T(4,128)(4,1)S(1)} %broadcast_compare_fusion), kind=kOutput, calls=%fused_computation.32 | convolution fusion | flops 3226009600 | bytes 12719104 | tf_op jit(solution)/shard_map/jcd,jde->jce/dot_general | solution.py:320
  156.1 0.7 fusion.19
  156.8 0.9 fusion.8
  157.8 0.8 fusion.7
  158.6 0.7 fusion.26
  159.3 0.6 convolution_convert_fusion.2
  159.9 0.8 multiply_convert_fusion
  160.7 0.6 convolution_convert_fusion.5
  161.3 0.6 convolution_convert_fusion.3
  162.0 0.3 fusion.20
  162.3 12.1 %fusion.term_ref = bf16[256,8192]{1,0:T(8,128)(2,1)} fusion(bf16[5,8192,128]{2,1,0:T(8,128)(2,1)} %get-tuple-element.7, bf16[256,1,128]{2,0,1:T(8,128)(2,1)S(1)} %slice_bitcast_fusion, bf16[256,4,128]{2,0,1:T(8,128)(2,1)S(1)} %fusion.20), kind=kOutput, calls=%fused_computation.3 | convolution fusion | flops 2686615552 | bytes 15007744 | tf_op jit(solution)/shard_map/tje,jde->td/dot_general | solution.py:351
  174.4 0.8 pad_maximum_fusion.grads_ref
  175.2 94.3 %shard_map.87 = (bf16[7,256,1024]{2,1,0:T(8,128)(2,1)}, bf16[7,256,128]{2,1,0:T(8,128)(2,1)}, bf16[256,1024]{1,0:T(8,128)(2,1)}) custom-call(bf16[256,8192]{1,0:T(8,128)(2,1)} %fusion.term_ref, bf16[2,4,256,128]{3,2,1,0:T(8,128)(2,1)} %pad_maximum_fusion.grads_ref), custom_call_target="tpu_custom_call" | custom-call | tf_op jit(solution)/shard_map/pallas_call | solution.py:240
  269.5 2.9 %convert_reduce_fusion = f32[256,1024]{1,0:T(8,128)S(1)} fusion(bf16[7,256,1024]{2,1,0:T(8,128)(2,1)} %get-tuple-element.10), kind=kLoop, calls=%fused_computation.8 | loop fusion | flops 3407872 | bytes 4718592 | tf_op jit(solution)/shard_map/reduce_sum | solution.py:361
  272.4 2.0 add_convert_fusion
  274.4 0.1 convert_reduce_fusion.1
  274.5 0.7 convert_add_fusion
  (16 shorter events, 0.1 us)
Async XLA Ops:
  146.6 9.5 %copy-start = (bf16[2,1024,128]{2,1,0:T(8,128)(2,1)S(1)}, bf16[2,1024,128]{2,1,0:T(8,128)(2,1)}, u32[]{:S(2)}) copy-start(bf16[2,1024,128]{2,1,0:T(8,128)(2,1)} %get-tuple-element.8) | copy-start | bytes 1572868
  269.5 4.9 %copy-start.1 = (bf16[7,256,128]{2,1,0:T(8,128)(2,1)S(1)}, bf16[7,256,128]{2,1,0:T(8,128)(2,1)}, u32[]{:S(2)}) copy-start(bf16[7,256,128]{2,1,0:T(8,128)(2,1)} %get-tuple-element.11) | copy-start | bytes 1376260
